TPU v7x, 32 devices: a whole 2x2x4 slice. The times are simulated.
32 devices in a mesh: ep: 16 (over z, y, x), half: 2 (over core).
Axes of the slice: x: 2, y: 2, z: 4, core: 2. Of those that a mesh axis runs over, the one named last changes fastest.
Arguments:
- tokens: bfloat16 [2048, 2048], P('ep', 'half'), may hold values from -6 to 6
- gate_weights: float32 [2048, 8], P('ep'), may hold values from 0.05 to 0.3
- expert_ids: int32 [2048, 8], P('ep'), may hold values from 0 to 15, all different within a row; in each aligned block of 128 rows (0 to 127, 128 to 255, ...) at most 80 rows name the same one
- w_gate: bfloat16 [16, 2048, 768], P('ep', None, 'half'), may hold values from -0.125 to 0.125
- w_up: bfloat16 [16, 2048, 768], P('ep', None, 'half'), may hold values from -0.125 to 0.125
- w_down: bfloat16 [16, 768, 2048], P('ep', 'half'), may hold values from -0.21875 to 0.21875
Outputs:
- mixed: bfloat16 [2048, 2048], P('ep', 'half')
Inputs may be any that keep to these rules, and one draw needn't show every extreme that they name: `expert_ids`: each row names 8 different experts. Within the rows of one device (aligned blocks of 128 rows) no expert is named by more than 80 rows, and in every draw some expert is named by exactly 80 rows of some block.
All inputs are finite; a program needn't handle non-finite values.
Results may differ from a plain program's by a relative error of at most 0.0085.
Values may be sent and summed in bfloat16 or wider, within the bound.
A program may use at most 64 MiB of HBM per device.

v0:
```python
import jax
import jax.numpy as jnp
from jax import lax
from jax.sharding import PartitionSpec as P


def local(tokens, gate_weights, expert_ids, w_gate, w_up, w_down):
    tok_dev, half_width = tokens.shape
    top = expert_ids.shape[1]
    local_experts = w_gate.shape[0]
    experts = local_experts * lax.axis_size("ep")
    capacity = min(tok_dev, max(2, 5 * tok_dev * top // (4 * experts)))
    flat_ids = expert_ids.reshape(-1)
    columns = jnp.arange(experts, dtype=jnp.int32)
    onehot = (flat_ids[:, None] == columns[None, :]).astype(jnp.int32)
    ranks = jnp.sum((jnp.cumsum(onehot, axis=0) - onehot) * onehot, axis=1)
    slot = flat_ids * capacity + ranks
    token_of_pair = jnp.arange(tok_dev * top, dtype=jnp.int32) // top
    token_table = jnp.zeros((experts * capacity,), jnp.int32).at[slot].set(token_of_pair)
    filled = (
        jnp.zeros((experts * capacity,), jnp.bfloat16)
        .at[slot]
        .set(jnp.ones((tok_dev * top,), jnp.bfloat16))
    )
    outgoing = (tokens[token_table] * filled[:, None]).reshape(experts, capacity, half_width)
    received = lax.all_to_all(outgoing, "ep", split_axis=0, concat_axis=0, tiled=True)
    count = received.shape[1]
    whole = lax.all_gather(received, "half", axis=2, tiled=True)
    width = whole.shape[2]
    grouped = whole.reshape(-1, local_experts, count, width)
    gate = jnp.einsum("secd,edf->secf", grouped, w_gate, preferred_element_type=jnp.float32)
    up = jnp.einsum("secd,edf->secf", grouped, w_up, preferred_element_type=jnp.float32)
    hidden = (jax.nn.silu(gate) * up).astype(jnp.bfloat16)
    partial_out = jnp.einsum("secf,efd->secd", hidden, w_down, preferred_element_type=jnp.float32)
    partial_out = partial_out.astype(jnp.bfloat16).reshape(experts, count, width)
    widened = lax.optimization_barrier(partial_out).astype(jnp.float32)
    summed = lax.psum_scatter(widened.astype(jnp.bfloat16), "half", scatter_dimension=2, tiled=True)
    answer = lax.all_to_all(summed, "ep", split_axis=0, concat_axis=0, tiled=True)
    picked = answer.reshape(experts * capacity, -1)[slot].reshape(tok_dev, top, -1)
    slot_out = picked.astype(jnp.float32)
    mixed = jnp.einsum("tk,tkx->tx", gate_weights, slot_out)
    return mixed.astype(jnp.bfloat16)


def solution(mesh):
    placed = (
        P("ep", "half"),
        P("ep", None),
        P("ep", None),
        P("ep", None, "half"),
        P("ep", None, "half"),
        P("ep", "half", None),
    )
    return jax.shard_map(
        local, mesh=mesh, in_specs=placed, out_specs=P("ep", "half"), check_vma=False
    )
```

profile of v0, /device:TPU:14, one launch (start us, length us, event | category | flops | bytes accessed | tf_op | source)
XLA Modules:
  0.0 229.0 jit_solution(11621073535470080937)
XLA Ops:
  6.5 0.9 copy.10
  7.5 0.1 eq.29
  7.6 0.1 eq.25
  7.6 0.7 broadcast_multiply_fusion.1
  8.4 4.5 %reduce-window.6 = s32[16,8,128]{2,1,0:T(8,128)S(1)} reduce-window(s32[16,8,128]{2,1,0:T(8,128)S(1)} %fusion.18, s32[]{:T(128)} %constant.27.clone.1), window={size=1x1x128 pad=0_0x0_0x127_0}, to_apply=%region_0.0 | reduce-window | flops 2080768 | bytes 131076 | tf_op jit(solution)/shard_map/reduce-window
  12.9 0.1 slice.12
  12.9 0.1 copy.12
  13.1 0.1 copy.13
  13.2 0.1 broadcast_add_fusion
  13.3 0.1 copy.9
  13.4 0.1 mul.39
  13.5 4.3 %scatter_custom_fusion = s32[1280]{0:T(1024)S(1)} fusion(s32[1024]{0:T(1024)S(1)} %bitcast.89, s32[1024]{0:T(1024)S(1)} %add_select_fusion, s32[]{:T(128)} %constant.27.clone.1), kind=kCustom, calls=%fused_computation.38 | custom fusion | bytes 5124 | tf_op jit(solution)/shard_map/scatter | solution.py:19
  17.9 7.6 %scatter_custom_fusion.1 = bf16[1280]{0:T(1024)(128)(2,1)S(1)} fusion(s32[1024]{0:T(1024)S(1)} %bitcast.90, bf16[1024]{0:T(1024)(128)(2,1)S(1)} %broadcast.65, bf16[]{:T(256)} %constant.35.clone.1), kind=kCustom, calls=%fused_computation.42 | custom fusion | bytes 2562 | tf_op jit(solution)/shard_map/scatter | solution.py:23
  25.5 0.1 mul.41
  25.6 0.0 copy-done.1
  25.6 5.1 %gather_fusion = bf16[1280,1024]{1,0:T(8,128)(2,1)} fusion(bf16[128,1024]{1,0:T(8,128)(2,1)S(1)} %copy-done.1, s32[2048]{0:T(1024)S(1)} %pad_clamp_fusion), kind=kCustom, calls=%fused_computation | custom fusion | bytes 5248000 | tf_op jit(solution)/shard_map/gather | solution.py:25
  30.7 2.0 broadcast_multiply_fusion
  32.7 65.0 %all_to_all.10 = bf16[16,80,1024]{2,1,0:T(8,128)(2,1)} all-to-all(bf16[16,80,1024]{2,1,0:T(8,128)(2,1)S(1)} %broadcast_multiply_fusion), channel_id=1, replica_groups=mesh['ep'=16,'half'=2] {'ep'}, dimensions={0} | all-to-all | bytes 5242880 | tf_op jit(solution)/shard_map/all_to_all | solution.py:26
  97.7 0.0 all-gather.2.cloned.1.call-update
  97.7 0.0 reduce-scatter.2.cloned.1.call-start
  97.7 15.5 %all-gather.2.cloned.1.call-done = bf16[16,80,2048]{2,1,0:T(8,128)(2,1)} async-done(((bf16[16,80,1024]{2,1,0:T(8,128)(2,1)}), bf16[16,80,2048]{2,1,0:T(8,128)(2,1)}) %all-gather.2.cloned.1.call-update) | async-done | bytes 5242896 | tf_op jit(solution)/shard_map/all_gather | solution.py:28
  113.3 6.6 %fusion.8 = f32[16,80,384]{2,1,0:T(8,128)} fusion(bf16[16,80,2048]{2,1,0:T(8,128)(2,1)} %all-gather.2.cloned.1.call-done, bf16[1,2048,384]{2,1,0:T(8,128)(2,1)S(1)} %copy-done.3), kind=kOutput, calls=%fused_computation.16 | convolution fusion | flops 2013265920 | bytes 8781824 | tf_op jit(solution)/shard_map/secd,edf->secf/dot_general | solution.py:31
  119.9 9.9 %convolution_convert_fusion = bf16[16,80,2048]{2,1,0:T(8,128)(2,1)} fusion(bf16[1,384,2048]{2,1,0:T(8,128)(2,1)S(1)} %copy-done, bf16[16,80,2048]{2,1,0:T(8,128)(2,1)} %all-gather.2.cloned.1.call-done, bf16[1,2048,384]{2,1,0:T(8,128)(2,1)} %param.10, f32[16,80,384]{2,1,0:T(8,128)} %fusion.8), kind=kOutput, calls=%fused_computation.4 | convolution fusion | flops 4032102400 | bytes 15597568 | tf_op jit(solution)/shard_map/secf,efd->secd/dot_general | solution.py:34
  129.8 0.0 reduce-scatter.2.cloned.1.call-update
  129.8 0.0 copy-start.2
  129.8 14.3 %reduce-scatter.2.cloned.1.call-done = bf16[16,80,1024]{2,1,0:T(8,128)(2,1)} async-done(((bf16[16,80,2048]{2,1,0:T(8,128)(2,1)}), bf16[16,80,1024]{2,1,0:T(8,128)(2,1)}) %reduce-scatter.2.cloned.1.call-update) | async-done | bytes 2621456 | tf_op jit(solution)/shard_map/reduce_scatter | solution.py:37
  144.1 7.0 %all-to-all-start.1 = ((bf16[16,80,1024]{2,1,0:T(8,128)(2,1)}), bf16[16,80,1024]{2,1,0:T(8,128)(2,1)}, u32[]{:S(2)}, u32[]{:S(2)}) async-start(bf16[16,80,1024]{2,1,0:T(8,128)(2,1)} %reduce-scatter.2.cloned.1.call-done), calls=%async_computation.2 | async-start | bytes 5242880 | tf_op jit(solution)/shard_map/all_to_all | solution.py:38
  151.1 0.1 copy.14
  151.3 59.8 %all-to-all-done.1 = bf16[16,80,1024]{2,1,0:T(8,128)(2,1)} async-done(((bf16[16,80,1024]{2,1,0:T(8,128)(2,1)}), bf16[16,80,1024]{2,1,0:T(8,128)(2,1)}, u32[]{:S(2)}, u32[]{:S(2)}) %all-to-all-start.1) | async-done | bytes 2621472 | tf_op jit(solution)/shard_map/all_to_all | solution.py:38
  211.0 8.1 %gather_fusion.1 = bf16[1024,1024]{1,0:T(8,128)(2,1)} fusion(bf16[1280,1024]{1,0:T(8,128)(2,1)} %bitcast.20, s32[1024]{0:T(1024)S(1)} %broadcast_clamp_fusion), kind=kCustom, calls=%fused_computation.1 | custom fusion | bytes 4198400 | tf_op jit(solution)/shard_map/gather | solution.py:39
  219.1 2.3 fusion
  221.4 0.8 copy.19
  (17 shorter events, 0.1 us)
Async XLA Ops:
  6.5 113.4 %copy-start = (bf16[1,384,2048]{2,1,0:T(8,128)(2,1)S(1)}, bf16[1,384,2048]{2,1,0:T(8,128)(2,1)}, u32[]{:S(2)}) copy-start(bf16[1,384,2048]{2,1,0:T(8,128)(2,1)} %param.11) | copy-start | bytes 4718596
  6.5 19.0 %copy-start.1 = (bf16[128,1024]{1,0:T(8,128)(2,1)S(1)}, bf16[128,1024]{1,0:T(8,128)(2,1)}, u32[]{:S(2)}) copy-start(bf16[128,1024]{1,0:T(8,128)(2,1)} %param.6) | copy-start | bytes 786436
  6.5 106.7 %all-gather.2.cloned.1.call-start = ((), (), s32[]{:S(2)}) async-start(), calls=%async_computation.3 | async-start | bytes 7864320 | tf_op jit(solution)/shard_map/all_gather | solution.py:28
  97.7 15.6 %copy-start.3 = (bf16[1,2048,384]{2,1,0:T(8,128)(2,1)S(1)}, bf16[1,2048,384]{2,1,0:T(8,128)(2,1)}, u32[]{:S(2)}) copy-start(bf16[1,2048,384]{2,1,0:T(8,128)(2,1)} %param.9) | copy-start | bytes 4718596
  97.7 46.4 %reduce-scatter.2.cloned.1.call-start = ((), (), s32[]{:S(2)}) async-start(), calls=%async_computation.4 | async-start | bytes 7864320 | tf_op jit(solution)/shard_map/reduce_scatter | solution.py:37
  129.8 21.3 %copy-start.2 = (f32[128,8]{0,1:T(8,128)S(1)}, f32[128,8]{0,1:T(8,128)}, u32[]{:S(2)}) copy-start(f32[128,8]{0,1:T(8,128)} %param.7) | copy-start | bytes 12292
  144.1 66.9 %all-to-all-start.1 = ((bf16[16,80,1024]{2,1,0:T(8,128)(2,1)}), bf16[16,80,1024]{2,1,0:T(8,128)(2,1)}, u32[]{:S(2)}, u32[]{:S(2)}) async-start(bf16[16,80,1024]{2,1,0:T(8,128)(2,1)} %reduce-scatter.2.cloned.1.call-done), calls=%async_computation.2 | async-start | bytes 5242880 | tf_op jit(solution)/shard_map/all_to_all | solution.py:38
Sparse Core Ops, SparseCore 0:
  97.8 15.4 all-gather.1
  129.9 14.1 reduce-scatter.1
where the time goes:
time: 229 us
  waiting for transfers between devices  89.6 us (39%)
  blocking collectives  65 us (28%)
  local copies, waits for them, and re-layouts  27.7 us (12%)
  matrix products  18.8 us (8%)
  between operations  13.5 us (6%)
  other arithmetic  7.36 us (3%)
  starting transfers between devices  7.01 us (3%)
    all_to_all x1, blocking collectives, local(): lax.all_to_all(outgoing, 'ep', split_axis=0, concat_axis=0, tiled=True)  65 us
    all_to_all x1, waiting for transfers between devices, local(): lax.all_to_all(summed, 'ep', split_axis=0, concat_axis=0, tiled=True)  59.8 us
    all_gather x1, waiting for transfers between devices, local(): whole = lax.all_gather(received, 'half', axis=2, tiled=True)  15.5 us
    reduce_scatter x1, waiting for transfers between devices, local(): lax.psum_scatter(widened.astype(jnp.bfloat16), 'half', scatter_dimension=...  14.3 us
    dot_general x1, matrix products, local(): jnp.einsum('secf,efd->secd', hidden, w_down, preferred_element_type=jnp.f...  9.86 us
    gather x1, local copies, waits for them, and re-layouts, local(): answer.reshape(experts * capacity, -1)[slot].reshape(tok_dev, top, -1)  8.11 us
    scatter x1, local copies, waits for them, and re-layouts, local(): filled = jnp.zeros((experts * capacity,), jnp.bfloat16).at[slot].set(jnp....  7.59 us
    all_to_all x1, starting transfers between devices, local(): lax.all_to_all(summed, 'ep', split_axis=0, concat_axis=0, tiled=True)  6.96 us
  transfers between devices with their start and end apart: 3, of which 3 were waited for; matrix products, arithmetic and copies ran while one was open for 0% of the time, Pallas kernels for 0%

commit v1 on v0

--- a/solution.py
+++ b/solution.py
@@ -1,10 +1,16 @@
+import functools
+
 import jax
 import jax.numpy as jnp
 from jax import lax
+from jax.experimental import pallas as pl
+from jax.experimental.pallas import tpu as pltpu
 from jax.sharding import PartitionSpec as P
 
-
-def local(tokens, gate_weights, expert_ids, w_gate, w_up, w_down):
+MESH = pl.DeviceIdType.MESH
+
+
+def slots(tokens, gate_weights, expert_ids, w_gate, w_up, w_down):
     tok_dev, half_width = tokens.shape
     top = expert_ids.shape[1]
     local_experts = w_gate.shape[0]
@@ -42,6 +48,234 @@
     return mixed.astype(jnp.bfloat16)
 
 
+def kernel(nz, tok_ref, gw_ref, ids_ref, wg_ref, wu_ref, wd_ref, out_ref,
+           xg, wgu, wdn, pa, pb, da, db, rxa, rxb, rya, ryb, own, zs, rz, fin, rfin,
+           load_sem, pre_sem, wsend, wrecv, zsend, zrecv, xsend, xrecv, ysend, yrecv,
+           fxsend, fxrecv, fysend, fyrecv,
+           esend, erecv, dsend, drecv, csend, crecv, qsend, qrecv, fsend, frecv):
+    ep = lax.axis_index("ep")
+    core = lax.axis_index("half")
+    x, y, z = ep % 2, (ep // 2) % 2, ep // 4
+    rows, width = out_ref.shape[0] // 2, wg_ref.shape[1]
+    half, ff = width // 2, wg_ref.shape[2]
+    other = {"half": 1 - core}
+    xn = {"ep": z * 4 + y * 2 + (1 - x)}
+    yn = {"ep": z * 4 + (1 - y) * 2 + x}
+
+    def zn(to):
+        return {"ep": to * 4 + y * 2 + x}
+
+    def send(src, dst, s, r, to):
+        return pltpu.make_async_remote_copy(
+            src_ref=src, dst_ref=dst, send_sem=s, recv_sem=r, device_id=to, device_id_type=MESH
+        )
+
+    def at(d):
+        return (z + nz - d) % nz
+
+    loads = [
+        pltpu.make_async_copy(wg_ref.at[0], wgu.at[0, :, pl.ds(0, ff)], load_sem.at[0]),
+        pltpu.make_async_copy(wu_ref.at[0], wgu.at[0, :, pl.ds(ff, ff)], load_sem.at[1]),
+        pltpu.make_async_copy(wd_ref.at[0], wdn.at[pl.ds(0, ff)], load_sem.at[2]),
+    ]
+    mine = pltpu.make_async_copy(
+        tok_ref.at[pl.ds(core * rows, rows)],
+        xg.at[0, z, :, pl.ds(pl.multiple_of(core * half, 128), half)],
+        load_sem.at[3],
+    )
+    mine.start()
+    for load in loads:
+        load.start()
+
+    lane = lax.broadcasted_iota(jnp.int32, (rows, 128), 1)
+    spread = jnp.zeros((rows, 128), jnp.float32)
+    ids = ids_ref[pl.ds(core * rows, rows), :]
+    weights = gw_ref[pl.ds(core * rows, rows), :]
+    for k in range(ids.shape[1]):
+        spread += jnp.where(lane % 64 == ids[:, k : k + 1], weights[:, k : k + 1], 0.0)
+    upper = spread.astype(jnp.bfloat16).astype(jnp.float32)
+    both = jnp.where(lane < 64, upper, spread - upper)
+    xg[0, z, :, width : width + 128] = both.astype(jnp.bfloat16)
+
+    barrier = pltpu.get_barrier_semaphore()
+    partners = [other, xn, yn] + [zn(at(d)) for d in range(1, nz)]
+    for partner in partners:
+        pl.semaphore_signal(barrier, inc=1, device_id=partner, device_id_type=MESH)
+    pl.semaphore_wait(barrier, len(partners))
+
+    pre = send(
+        tok_ref.at[pl.ds((1 - core) * rows, rows)],
+        xg.at[0, z, :, pl.ds(pl.multiple_of(core * half, 128), half)],
+        pre_sem.at[0], pre_sem.at[1], other,
+    )
+    pre.start()
+    swaps = [
+        send(wg_ref.at[0], wgu.at[1, :, pl.ds(0, ff)], wsend.at[0], wrecv.at[0], other),
+        send(wu_ref.at[0], wgu.at[1, :, pl.ds(ff, ff)], wsend.at[1], wrecv.at[1], other),
+        send(wd_ref.at[0], wdn.at[pl.ds(ff, ff)], wsend.at[2], wrecv.at[2], other),
+    ]
+    mine.wait()
+    pre.wait_recv()
+    sent = [pre]
+
+    def go(copy):
+        copy.start()
+        sent.append(copy)
+        return copy
+
+    first, last = pl.ds(0, half), pl.ds(half, half + 128)
+    xs, ys, fx, fy, zc = {}, {}, {}, {}, {}
+
+    def column(d):
+        b = xg.at[0, at(d)]
+        xs[d] = go(send(b, xg.at[1, at(d)], xsend.at[d], xrecv.at[d], xn))
+        ys[d] = go(send(b, xg.at[2, at(d)], ysend.at[d], yrecv.at[d], yn))
+
+    def forward(d):
+        ys[d].wait_recv()
+        fx[d] = go(send(xg.at[2, at(d), :, last], xg.at[3, at(d), :, last],
+                        fxsend.at[d], fxrecv.at[d], xn))
+        xs[d].wait_recv()
+        fy[d] = go(send(xg.at[1, at(d), :, first], xg.at[3, at(d), :, first],
+                        fysend.at[d], fyrecv.at[d], yn))
+
+    for d in range(1, nz):
+        zc[d] = go(send(xg.at[0, z], xg.at[0, z], zsend.at[d - 1], zrecv.at[d - 1], zn((z + d) % nz)))
+    column(0)
+    for swap in swaps:
+        go(swap)
+    for d in range(1, nz):
+        zc[d].wait_recv()
+        column(d)
+        forward(d - 1)
+
+    many = nz * rows
+
+    def expert(g):
+        lanes = lax.broadcasted_iota(jnp.int32, (many, 128), 1)
+        table = xg[g, :, :, width : width + 128].reshape(many, 128).astype(jnp.float32)
+        weight = jnp.sum(jnp.where(lanes % 64 == ep, table, 0.0), axis=1, keepdims=True)
+        rows_in = xg[g, :, :, 0:width].reshape(many, width)
+        parts = []
+        for side in range(2):
+            gu = jnp.dot(rows_in, wgu[side], preferred_element_type=jnp.float32)
+            gate, up = gu[:, :ff], gu[:, ff:]
+            hid = gate / (1.0 + jnp.exp(-gate)) * up * weight
+            parts.append(hid.astype(jnp.bfloat16))
+        hidden = jnp.concatenate(parts, axis=1)
+        for to, start in ((pa, 0), (pb, half)):
+            o = jnp.dot(hidden, wdn[:, start : start + half], preferred_element_type=jnp.float32)
+            to[g] = o.astype(jnp.bfloat16).reshape(nz, rows, half)
+
+    for load in loads:
+        load.wait()
+    for swap in swaps:
+        swap.wait_recv()
+    expert(0)
+    forward(nz - 1)
+    expert(1)
+    early_x = go(send(pb.at[1], rxb, esend.at[0], erecv.at[0], xn))
+    expert(2)
+    early_y = go(send(pa.at[2], rya, esend.at[1], erecv.at[1], yn))
+    for d in range(nz):
+        fx[d].wait_recv()
+        fy[d].wait_recv()
+    expert(3)
+    order = list(range(1, nz)) + [0]
+    dx, dy, cx, cy, zq = {}, {}, {}, {}, {}
+    for d in order:
+        dy[d] = go(send(pa.at[3, at(d)], da.at[at(d)], dsend.at[0, d], drecv.at[0, d], yn))
+        dx[d] = go(send(pb.at[3, at(d)], db.at[at(d)], dsend.at[1, d], drecv.at[1, d], xn))
+    f32 = jnp.float32
+    for d in order:
+        dy[d].wait_recv()
+        pa[1, at(d)] = (pa[1, at(d)].astype(f32) + da[at(d)].astype(f32)).astype(jnp.bfloat16)
+        cx[d] = go(send(pa.at[1, at(d)], rxa.at[at(d)], csend.at[0, d], crecv.at[0, d], xn))
+        dx[d].wait_recv()
+        pb[2, at(d)] = (pb[2, at(d)].astype(f32) + db[at(d)].astype(f32)).astype(jnp.bfloat16)
+        cy[d] = go(send(pb.at[2, at(d)], ryb.at[at(d)], csend.at[1, d], crecv.at[1, d], yn))
+    early_x.wait_recv()
+    early_y.wait_recv()
+    for d in order:
+        cx[d].wait_recv()
+        cy[d].wait_recv()
+        sums = []
+        for p, u, v in ((pa, rxa, rya), (pb, rxb, ryb)):
+            sums.append(p[0, at(d)].astype(f32) + u[at(d)].astype(f32) + v[at(d)].astype(f32))
+        if d:
+            zs[d - 1, :, 0:half] = sums[0].astype(jnp.bfloat16)
+            zs[d - 1, :, half:width] = sums[1].astype(jnp.bfloat16)
+            zq[d] = go(send(zs.at[d - 1], rz.at[d - 1], qsend.at[d - 1], qrecv.at[d - 1], zn(at(d))))
+        else:
+            own[:, 0:half] = sums[0]
+            own[:, half:width] = sums[1]
+    total = own[...]
+    for d in range(1, nz):
+        zq[d].wait_recv()
+        total += rz[d - 1].astype(f32)
+    total = total.astype(jnp.bfloat16)
+    fin[0] = total[:, 0:half]
+    fin[1] = total[:, half:width]
+    swap = go(send(fin.at[1 - core], rfin, fsend, frecv, other))
+    out_ref[pl.ds(core * rows, rows), :] = fin[core]
+    swap.wait_recv()
+    out_ref[pl.ds((1 - core) * rows, rows), :] = rfin[...]
+    for copy in sent:
+        copy.wait_send()
+
+
+def multicast(tokens, gate_weights, expert_ids, w_gate, w_up, w_down):
+    tok_dev, half = tokens.shape
+    nz = lax.axis_size("ep") // 4
+    rows, width, ff = tok_dev // 2, w_gate.shape[1], w_gate.shape[2]
+    bf, dma = jnp.bfloat16, pltpu.SemaphoreType.DMA
+    vmem, hbm = pl.BlockSpec(memory_space=pltpu.VMEM), pl.BlockSpec(memory_space=pl.ANY)
+    return pl.pallas_call(
+        functools.partial(kernel, nz),
+        out_shape=jax.ShapeDtypeStruct((tok_dev, half), bf),
+        in_specs=[vmem, vmem, vmem, hbm, hbm, hbm],
+        out_specs=vmem,
+        scratch_shapes=[
+            pltpu.VMEM((4, nz, rows, width + 128), bf),
+            pltpu.VMEM((2, width, 2 * ff), bf),
+            pltpu.VMEM((2 * ff, width), bf),
+            pltpu.VMEM((4, nz, rows, half), bf),
+            pltpu.VMEM((4, nz, rows, half), bf),
+            pltpu.VMEM((nz, rows, half), bf),
+            pltpu.VMEM((nz, rows, half), bf),
+            pltpu.VMEM((nz, rows, half), bf),
+            pltpu.VMEM((nz, rows, half), bf),
+            pltpu.VMEM((nz, rows, half), bf),
+            pltpu.VMEM((nz, rows, half), bf),
+            pltpu.VMEM((rows, width), jnp.float32),
+            pltpu.VMEM((nz - 1, rows, width), bf),
+            pltpu.VMEM((nz - 1, rows, width), bf),
+            pltpu.VMEM((2, rows, half), bf),
+            pltpu.VMEM((rows, half), bf),
+            dma((4,)), dma((2,)), dma((3,)), dma((3,)),
+            dma((nz - 1,)), dma((nz - 1,)),
+            dma((nz,)), dma((nz,)), dma((nz,)), dma((nz,)),
+            dma((nz,)), dma((nz,)), dma((nz,)), dma((nz,)),
+            dma((2,)), dma((2,)), dma((2, nz)), dma((2, nz)), dma((2, nz)), dma((2, nz)),
+            dma((nz - 1,)), dma((nz - 1,)), dma, dma,
+        ],
+        compiler_params=pltpu.CompilerParams(
+            collective_id=0, has_side_effects=True, vmem_limit_bytes=60 * 1024 * 1024
+        ),
+    )(tokens, gate_weights, expert_ids, w_gate, w_up, w_down)
+
+
+def local(tokens, gate_weights, expert_ids, w_gate, w_up, w_down):
+    tok_dev, half = tokens.shape
+    devices, cores = lax.axis_size("ep"), lax.axis_size("half")
+    experts = w_gate.shape[0] * devices
+    gathered = tok_dev * devices * half * 2
+    fits = gathered <= 8 * 1024 * 1024 and experts <= 64 and w_gate.shape[0] == 1
+    shaped = cores == 2 and devices % 4 == 0 and devices > 4 and tok_dev % 32 == 0
+    plan = multicast if fits and shaped else slots
+    return plan(tokens, gate_weights, expert_ids, w_gate, w_up, w_down)
+
+
 def solution(mesh):
     placed = (
         P("ep", "half"),

time: 229 us -> 109 us (0.48)
  the two profiles are of different devices: /device:TPU:14 before, /device:TPU:0 now
where the time goes in v1:
time: 109 us; the launch traced here: 108 us
  Pallas kernels  104 us (95%)
  local copies, waits for them, and re-layouts  4.49 us (4%)
    pallas_call x1, Pallas kernels, multicast(): pl.pallas_call(functools.partial(kernel, nz), out_shape=jax.ShapeDtypeStr...  104 us
    unnamed x3, local copies, waits for them, and re-layouts  4.49 us

profile of v1, /device:TPU:0, one launch (start us, length us, event | category | flops | bytes accessed | tf_op | source)
XLA Modules:
  0.0 108.3 jit_solution(6394599244111899038)
XLA Ops:
  0.0 1.4 %copy.7.gw_ref = f32[128,8]{1,0:T(8,128)} copy(f32[128,8]{0,1:T(8,128)} %param.7) | data formatting | bytes 8192 | tf_op args[1]
  1.4 1.4 %copy.8.ids_ref = s32[128,8]{1,0:T(8,128)} copy(s32[128,8]{0,1:T(8,128)} %param.8) | data formatting | bytes 8192 | tf_op args[2]
  2.8 103.8 %shard_map.64 = bf16[128,1024]{1,0:T(8,128)(2,1)} custom-call(bf16[128,1024]{1,0:T(8,128)(2,1)} %tok_ref.1, f32[128,8]{1,0:T(8,128)} %copy.7.gw_ref, s32[128,8]{1,0:T(8,128)} %copy.8.ids_ref, bf16[1,2048,384]{2,1,0:T(8,128)(2,1)} %wg_ref.1, bf16[1,2048,384]{2,1,0:T(8,128)(2,1)} %wu_ref.1, bf16[1,384,2048]{2,1,0:T(8,128)(2,1)} %wd_ref.1), custom_call_target="tpu_custom_call" | custom-call | tf_op jit(solution)/shard_map/pallas_call | solution.py:233
  106.7 1.7 %copy.10 = bf16[128,1024]{1,0:T(8,128)(2,1)} copy(bf16[128,1024]{1,0:T(8,128)(2,1)} %shard_map.64) | data formatting | bytes 524288

commit v2 on v1

--- a/solution.py
+++ b/solution.py
@@ -71,7 +71,12 @@
         )
 
     def at(d):
-        return (z + nz - d) % nz
+        bit, to = 1, z
+        while bit < nz:
+            if d & bit:
+                to = to + bit - 2 * bit * ((z // bit) % 2)
+            bit *= 2
+        return to
 
     loads = [
         pltpu.make_async_copy(wg_ref.at[0], wgu.at[0, :, pl.ds(0, ff)], load_sem.at[0]),
@@ -87,12 +92,13 @@
     for load in loads:
         load.start()
 
+    expert_at = lax.broadcasted_iota(jnp.int32, (128, 2 * rows), 0) % 64
+    spread = jnp.zeros((128, 2 * rows), jnp.float32)
+    for k in range(ids_ref.shape[0]):
+        spread += jnp.where(expert_at == ids_ref[k : k + 1, :], gw_ref[k : k + 1, :], 0.0)
+    spread = jnp.transpose(spread)
+    spread = jnp.where(core == 0, spread[:rows], spread[rows:])
     lane = lax.broadcasted_iota(jnp.int32, (rows, 128), 1)
-    spread = jnp.zeros((rows, 128), jnp.float32)
-    ids = ids_ref[pl.ds(core * rows, rows), :]
-    weights = gw_ref[pl.ds(core * rows, rows), :]
-    for k in range(ids.shape[1]):
-        spread += jnp.where(lane % 64 == ids[:, k : k + 1], weights[:, k : k + 1], 0.0)
     upper = spread.astype(jnp.bfloat16).astype(jnp.float32)
     both = jnp.where(lane < 64, upper, spread - upper)
     xg[0, z, :, width : width + 128] = both.astype(jnp.bfloat16)
@@ -128,26 +134,33 @@
 
     def column(d):
         b = xg.at[0, at(d)]
-        xs[d] = go(send(b, xg.at[1, at(d)], xsend.at[d], xrecv.at[d], xn))
-        ys[d] = go(send(b, xg.at[2, at(d)], ysend.at[d], yrecv.at[d], yn))
+        for p, cols in enumerate((first, last)):
+            xs[d, p] = go(send(b.at[:, cols], xg.at[1, at(d), :, cols],
+                               xsend.at[p, d], xrecv.at[p, d], xn))
+        for p, cols in ((1, last), (0, first)):
+            ys[d, p] = go(send(b.at[:, cols], xg.at[2, at(d), :, cols],
+                               ysend.at[p, d], yrecv.at[p, d], yn))
 
     def forward(d):
-        ys[d].wait_recv()
+        ys[d, 1].wait_recv()
         fx[d] = go(send(xg.at[2, at(d), :, last], xg.at[3, at(d), :, last],
                         fxsend.at[d], fxrecv.at[d], xn))
-        xs[d].wait_recv()
+        xs[d, 0].wait_recv()
         fy[d] = go(send(xg.at[1, at(d), :, first], xg.at[3, at(d), :, first],
                         fysend.at[d], fyrecv.at[d], yn))
 
-    for d in range(1, nz):
-        zc[d] = go(send(xg.at[0, z], xg.at[0, z], zsend.at[d - 1], zrecv.at[d - 1], zn((z + d) % nz)))
+    hops = sorted(range(1, nz), key=lambda d: bin(d ^ (d >> 1)).count("1"))
+    for d in hops:
+        zc[d] = go(send(xg.at[0, z], xg.at[0, z], zsend.at[d - 1], zrecv.at[d - 1], zn(at(d))))
     column(0)
     for swap in swaps:
         go(swap)
-    for d in range(1, nz):
+    forward(0)
+    for place, d in enumerate(hops):
         zc[d].wait_recv()
         column(d)
-        forward(d - 1)
+        if place:
+            forward(hops[place - 1])
 
     many = nz * rows
 
@@ -172,31 +185,36 @@
     for swap in swaps:
         swap.wait_recv()
     expert(0)
-    forward(nz - 1)
+    forward(hops[-1])
+    for d in range(nz):
+        xs[d, 1].wait_recv()
     expert(1)
     early_x = go(send(pb.at[1], rxb, esend.at[0], erecv.at[0], xn))
+    for d in range(nz):
+        ys[d, 0].wait_recv()
     expert(2)
     early_y = go(send(pa.at[2], rya, esend.at[1], erecv.at[1], yn))
     for d in range(nz):
         fx[d].wait_recv()
         fy[d].wait_recv()
     expert(3)
-    order = list(range(1, nz)) + [0]
+    order = hops[::-1] + [0]
     dx, dy, cx, cy, zq = {}, {}, {}, {}, {}
-    for d in order:
+    f32 = jnp.float32
+
+    def corner(d):
         dy[d] = go(send(pa.at[3, at(d)], da.at[at(d)], dsend.at[0, d], drecv.at[0, d], yn))
         dx[d] = go(send(pb.at[3, at(d)], db.at[at(d)], dsend.at[1, d], drecv.at[1, d], xn))
-    f32 = jnp.float32
-    for d in order:
+
+    def edge(d):
         dy[d].wait_recv()
         pa[1, at(d)] = (pa[1, at(d)].astype(f32) + da[at(d)].astype(f32)).astype(jnp.bfloat16)
         cx[d] = go(send(pa.at[1, at(d)], rxa.at[at(d)], csend.at[0, d], crecv.at[0, d], xn))
         dx[d].wait_recv()
         pb[2, at(d)] = (pb[2, at(d)].astype(f32) + db[at(d)].astype(f32)).astype(jnp.bfloat16)
         cy[d] = go(send(pb.at[2, at(d)], ryb.at[at(d)], csend.at[1, d], crecv.at[1, d], yn))
-    early_x.wait_recv()
-    early_y.wait_recv()
-    for d in order:
+
+    def home(d):
         cx[d].wait_recv()
         cy[d].wait_recv()
         sums = []
@@ -209,6 +227,19 @@
         else:
             own[:, 0:half] = sums[0]
             own[:, half:width] = sums[1]
+
+    corner(order[0])
+    corner(order[1])
+    for place, d in enumerate(order):
+        edge(d)
+        if place + 2 < len(order):
+            corner(order[place + 2])
+        if place == 1:
+            early_x.wait_recv()
+            early_y.wait_recv()
+        if place:
+            home(order[place - 1])
+    home(order[-1])
     total = own[...]
     for d in range(1, nz):
         zq[d].wait_recv()
@@ -254,7 +285,7 @@
             pltpu.VMEM((rows, half), bf),
             dma((4,)), dma((2,)), dma((3,)), dma((3,)),
             dma((nz - 1,)), dma((nz - 1,)),
-            dma((nz,)), dma((nz,)), dma((nz,)), dma((nz,)),
+            dma((2, nz)), dma((2, nz)), dma((2, nz)), dma((2, nz)),
             dma((nz,)), dma((nz,)), dma((nz,)), dma((nz,)),
             dma((2,)), dma((2,)), dma((2, nz)), dma((2, nz)), dma((2, nz)), dma((2, nz)),
             dma((nz - 1,)), dma((nz - 1,)), dma, dma,
@@ -262,7 +293,7 @@
         compiler_params=pltpu.CompilerParams(
             collective_id=0, has_side_effects=True, vmem_limit_bytes=60 * 1024 * 1024
         ),
-    )(tokens, gate_weights, expert_ids, w_gate, w_up, w_down)
+    )(tokens, gate_weights.T, expert_ids.T, w_gate, w_up, w_down)
 
 
 def local(tokens, gate_weights, expert_ids, w_gate, w_up, w_down):
@@ -271,7 +302,7 @@
     experts = w_gate.shape[0] * devices
     gathered = tok_dev * devices * half * 2
     fits = gathered <= 8 * 1024 * 1024 and experts <= 64 and w_gate.shape[0] == 1
-    shaped = cores == 2 and devices % 4 == 0 and devices > 4 and tok_dev % 32 == 0
+    shaped = cores == 2 and devices % 4 == 0 and devices > 4 and devices & (devices - 1) == 0 and tok_dev % 32 == 0
     plan = multicast if fits and shaped else slots
     return plan(tokens, gate_weights, expert_ids, w_gate, w_up, w_down)
 

time: 109 us -> 96.2 us (0.88)
  Pallas kernels: 104 us -> 94.4 us
  local copies, waits for them, and re-layouts: 4.49 us -> 1.67 us
    pallas_call x1, Pallas kernels: 104 us -> 94.4 us  [multicast(): pl.pallas_call(functools.partial(kernel, nz), out_shape=jax.ShapeDtypeStr...]
    unnamed x3 -> x1, local copies, waits for them, and re-layouts: 4.49 us -> 1.67 us
where the time goes in v2:
time: 96.2 us; the launch traced here: 96 us
  Pallas kernels  94.4 us (98%)
  local copies, waits for them, and re-layouts  1.67 us (2%)
    pallas_call x1, Pallas kernels, multicast(): pl.pallas_call(functools.partial(kernel, nz), out_shape=jax.ShapeDtypeStr...  94.4 us

profile of v2, /device:TPU:0, one launch (start us, length us, event | category | flops | bytes accessed | tf_op | source)
XLA Modules:
  0.0 96.0 jit_solution(17392221476247306335)
XLA Ops:
  0.0 94.4 %shard_map.64 = bf16[128,1024]{1,0:T(8,128)(2,1)} custom-call(bf16[128,1024]{1,0:T(8,128)(2,1)} %tok_ref.1, f32[8,128]{1,0:T(8,128)} %bitcast.2, s32[8,128]{1,0:T(8,128)} %bitcast.3, bf16[1,2048,384]{2,1,0:T(8,128)(2,1)} %wg_ref.1, bf16[1,2048,384]{2,1,0:T(8,128)(2,1)} %wu_ref.1, bf16[1,384,2048]{2,1,0:T(8,128)(2,1)} %wd_ref.1), custom_call_target="tpu_custom_call" | custom-call | tf_op jit(solution)/shard_map/pallas_call | solution.py:264
  94.4 1.7 %copy.8 = bf16[128,1024]{1,0:T(8,128)(2,1)} copy(bf16[128,1024]{1,0:T(8,128)(2,1)} %shard_map.64) | data formatting | bytes 524288
